TPU v7x, 32 devices: a whole 2x2x4 slice. The times are simulated.
32 devices in a mesh: dp: 4 (over x, core), fsdp: 2 (over y), tensor: 4 (over z).
Axes of the slice: x: 2, y: 2, z: 4, core: 2. Of those that a mesh axis runs over, the one named last changes fastest.
Arguments:
- tokens: bfloat16 [8, 768, 8192], P(('dp', 'fsdp'), 'tensor'), may hold values from -6 to 6
- norm_gain: float32 [8192], replicated, may hold values from 0.85 to 4
- w_qkv: bfloat16 [8192, 5120], P(('dp', 'fsdp'), 'tensor'), may hold values from -0.3 to 0.3
- a_query: bfloat16 [8192, 16], replicated, may hold values from -0.0625 to 0.0625
- query_up_adapter: bfloat16 [16, 4096], P(None, 'tensor'), may hold values from -1.5 to 1.5
- a_value: bfloat16 [8192, 16], replicated, may hold values from -0.0625 to 0.0625
- value_up_adapter: bfloat16 [16, 512], P(None, 'tensor'), may hold values from -1.5 to 1.5
- out_grad: bfloat16 [8, 768, 4096], P(('dp', 'fsdp'), 'tensor'), may hold values from -6 to 6
Outputs:
- attn_out: bfloat16 [8, 768, 4096], P(('dp', 'fsdp'), 'tensor')
- grad_a_query: float32 [8192, 16], replicated
- grad_b_query: float32 [16, 4096], P(None, 'tensor')
- grad_a_value: float32 [8192, 16], replicated
- grad_b_value: float32 [16, 512], P(None, 'tensor')
All inputs are finite; a program needn't handle non-finite values.
Results may differ from a plain program's by a relative error of at most 0.015.
The roundings to bfloat16 on the way count: a program that leaves them out, or rounds other values in their place, can miss the bound.
Values may be sent and summed in bfloat16 or wider, within the bound.
A program may use at most 256 MiB of HBM per device.

v0:
```python
import functools
import math

import jax
import jax.numpy as jnp
from jax import lax
from jax.experimental import pallas as pl
from jax.experimental.pallas import tpu as pltpu
from jax.sharding import PartitionSpec as P

HD = 128
QUERY_PER_KV = 8


EPSILON = 1e-05
ADAPTER_SCALE = 2.0
ROPE_BASE = 500000.0


def normalize(own_rows, norm_gain):
    widened = own_rows.astype(jnp.float32)
    mean_square = jnp.mean(widened * widened, axis=-1, keepdims=True)
    return (widened * lax.rsqrt(mean_square + EPSILON) * norm_gain).astype(jnp.bfloat16)


def rotary_tables(sequence_length):
    half_dim = HD // 2
    positions = jnp.arange(sequence_length, dtype=jnp.float32)[:, None]
    inv_freq = ROPE_BASE ** (-jnp.arange(half_dim, dtype=jnp.float32) / half_dim)
    angles = positions * inv_freq
    cosine, sine = jnp.cos(angles), jnp.sin(angles)
    return jnp.concatenate([cosine, cosine], 1), jnp.concatenate([-sine, sine], 1)


def dot(a, b, dims):
    return lax.dot_general(a, b, (dims, ((), ())), preferred_element_type=jnp.float32)


def attention_kernel(
    block, q_ref, k_ref, v_ref, dq_ref, dv_ref, qup_ref, vup_ref, cos_ref, sin_ref, g_ref,
    out_ref, gbq_ref, gbv_ref, midq_ref, midv_ref,
    keys, values, value_grad, query_grad,
):
    group, head = pl.program_id(0), pl.program_id(1)
    heads = pl.num_programs(1)
    length = q_ref.shape[0]
    scale = 1.0 / math.sqrt(HD)

    @pl.when(head == 0)
    def _():
        k = k_ref[...].astype(jnp.bfloat16).astype(jnp.float32)
        keys[...] = (k * cos_ref[...] + pltpu.roll(k, HD // 2, 1) * sin_ref[...]).astype(jnp.bfloat16)
        values[...] = (
            v_ref[...] + ADAPTER_SCALE * dot(dv_ref[...], vup_ref[...], ((1,), (0,)))
        ).astype(jnp.bfloat16)
        value_grad[...] = jnp.zeros_like(value_grad)

    @pl.when((head == 0) & (group == 0))
    def _():
        midq_ref[...] = jnp.zeros_like(midq_ref)
        midv_ref[...] = jnp.zeros_like(midv_ref)

    for start in range(0, length, block):
        rows = pl.ds(start, block)
        reach = start + block
        q = (
            q_ref[rows, :] + ADAPTER_SCALE * dot(dq_ref[rows, :], qup_ref[...], ((1,), (0,)))
        ).astype(jnp.bfloat16).astype(jnp.float32)
        cosine, sine = cos_ref[rows, :], sin_ref[rows, :]
        turned = (q * cosine + pltpu.roll(q, HD // 2, 1) * sine).astype(jnp.bfloat16)
        k, v, g = keys[pl.ds(0, reach), :], values[pl.ds(0, reach), :], g_ref[rows, :]
        scores = dot(turned, k, ((1,), (1,))) * scale
        row = lax.broadcasted_iota(jnp.int32, scores.shape, 0) + start
        col = lax.broadcasted_iota(jnp.int32, scores.shape, 1)
        scores = jnp.where(row >= col, scores, -1e30)
        weights = jnp.exp(scores - jnp.max(scores, axis=-1, keepdims=True))
        wide = weights * (1.0 / jnp.sum(weights, axis=-1, keepdims=True))
        probabilities = wide.astype(jnp.bfloat16)
        out_ref[rows, :] = dot(probabilities, v, ((1,), (0,))).astype(jnp.bfloat16)
        value_grad[pl.ds(0, reach), :] += dot(probabilities, g, ((0,), (0,)))
        prob_grad = dot(g, v, ((1,), (1,)))
        inner = jnp.sum(prob_grad * wide, axis=-1, keepdims=True)
        score_grad = (wide * (prob_grad - inner) * scale).astype(jnp.bfloat16)
        turned_grad = dot(score_grad, k, ((1,), (0,))).astype(jnp.bfloat16).astype(jnp.float32)
        query_grad[rows, :] = (
            turned_grad * cosine - pltpu.roll(turned_grad, HD // 2, 1) * sine
        ).astype(jnp.bfloat16)

    gq = query_grad[...]
    gbq_ref[...] = ADAPTER_SCALE * dot(dq_ref[...], gq, ((0,), (0,)))
    midq_ref[...] += dot(gq, qup_ref[...], ((1,), (1,)))

    @pl.when(head == heads - 1)
    def _():
        gv = value_grad[...].astype(jnp.bfloat16)
        gbv_ref[...] = ADAPTER_SCALE * dot(dv_ref[...], gv, ((0,), (0,)))
        midv_ref[...] += dot(gv, vup_ref[...], ((1,), (1,)))


def attention(projected, down_q, down_v, query_up, value_up, grad_rows):
    length, cols = projected.shape
    rank = down_q.shape[1]
    per = QUERY_PER_KV + 2
    groups = cols // (per * HD)
    block = 256 if length % 256 == 0 else length
    cosine, sine = rotary_tables(length)
    heads = groups * QUERY_PER_KV
    whole = lambda shape: pl.BlockSpec(shape, lambda g, h: (0, 0))
    column = lambda n, index: pl.BlockSpec((n, HD), lambda g, h: (0, index(g, h)))
    by_head = lambda g, h: g * QUERY_PER_KV + h
    return pl.pallas_call(
        functools.partial(attention_kernel, block),
        grid=(groups, QUERY_PER_KV),
        in_specs=[
            column(length, lambda g, h: g * per + h),
            column(length, lambda g, h: g * per + QUERY_PER_KV),
            column(length, lambda g, h: g * per + QUERY_PER_KV + 1),
            whole((length, rank)),
            whole((length, rank)),
            column(rank, by_head),
            column(rank, lambda g, h: g),
            whole((length, HD)),
            whole((length, HD)),
            column(length, by_head),
        ],
        out_specs=[
            column(length, by_head),
            column(rank, by_head),
            column(rank, lambda g, h: g),
            whole((length, rank)),
            whole((length, rank)),
        ],
        out_shape=[
            jax.ShapeDtypeStruct((length, heads * HD), jnp.bfloat16),
            jax.ShapeDtypeStruct((rank, heads * HD), jnp.float32),
            jax.ShapeDtypeStruct((rank, groups * HD), jnp.float32),
            jax.ShapeDtypeStruct((length, rank), jnp.float32),
            jax.ShapeDtypeStruct((length, rank), jnp.float32),
        ],
        scratch_shapes=[
            pltpu.VMEM((length, HD), jnp.bfloat16),
            pltpu.VMEM((length, HD), jnp.bfloat16),
            pltpu.VMEM((length, HD), jnp.float32),
            pltpu.VMEM((length, HD), jnp.bfloat16),
        ],
        compiler_params=pltpu.CompilerParams(
            dimension_semantics=("arbitrary", "arbitrary"), vmem_limit_bytes=48 * 2**20
        ),
        cost_estimate=pl.CostEstimate(
            flops=10 * heads * length * length * HD,
            bytes_accessed=length * cols * 4 + 2 * length * heads * HD * 2,
            transcendentals=heads * length * length,
        ),
        name="attention",
    )(projected, projected, projected, down_q, down_v, query_up, value_up, cosine, sine, grad_rows)


def local(count, tokens, norm_gain, w_qkv, a_query, query_up_adapter, a_value, value_up_adapter, out_grad):
    own = normalize(tokens[0], norm_gain)
    own_rows = own.shape[0]
    rank = a_query.shape[1]
    place = lax.axis_index("tensor")
    weights = lax.all_gather(w_qkv, ("dp", "fsdp"), axis=0, tiled=True)
    adapters = jnp.concatenate([a_query, a_value], 1)
    grad_rows = lax.all_to_all(out_grad[0], "tensor", split_axis=1, concat_axis=0, tiled=True)

    down_own = jnp.dot(own, adapters, preferred_element_type=jnp.float32).astype(jnp.bfloat16)
    down_projected = lax.all_gather(down_own, "tensor", axis=0, tiled=True)

    upward, downward = [], []
    up_block = down_block = own
    for step in range(1, count):
        if step > 1 and step == count - 1:
            up_block, down_block, weights = lax.optimization_barrier((up_block, down_block, weights))
            upward[-1], downward[-1] = up_block, down_block
        up_block = lax.ppermute(up_block, "tensor", [(i, i + 1) for i in range(step - 1, count - 1)])
        down_block = lax.ppermute(down_block, "tensor", [(i, i - 1) for i in range(1, count - step + 1)])
        upward.append(up_block)
        downward.append(down_block)
    blocks = [
        jnp.dot(rows, weights, preferred_element_type=jnp.float32)
        for rows in upward[::-1] + [own] + downward
    ]
    window = (count - 1 - place) * own_rows
    projected = lax.dynamic_slice_in_dim(jnp.concatenate(blocks, 0), window, count * own_rows, 0)
    attended, query_up_gradient, value_up_gradient, mid_query, mid_value = attention(
        projected, down_projected[:, :rank], down_projected[:, rank:],
        query_up_adapter, value_up_adapter, grad_rows,
    )
    out_rows = lax.all_to_all(attended, "tensor", split_axis=0, concat_axis=1, tiled=True)
    mid_own = lax.psum_scatter(
        jnp.concatenate([mid_query, mid_value], 1), "tensor", scatter_dimension=0, tiled=True
    ).astype(jnp.bfloat16)
    down_gradient = ADAPTER_SCALE * jnp.einsum(
        "uh,ux->xh", own, mid_own, preferred_element_type=jnp.float32
    )
    down_gradient = lax.psum(down_gradient, ("dp", "fsdp", "tensor")).T
    query_up_gradient, value_up_gradient = lax.psum(
        (query_up_gradient, value_up_gradient), ("dp", "fsdp")
    )
    return (
        out_rows[None],
        down_gradient[:, :rank],
        query_up_gradient,
        down_gradient[:, rank:],
        value_up_gradient,
    )


def solution(mesh):
    return jax.shard_map(
        functools.partial(local, mesh.shape["tensor"]),
        mesh=mesh,
        in_specs=(
            P(("dp", "fsdp"), "tensor", None),
            P(),
            P(("dp", "fsdp"), "tensor"),
            P(),
            P(None, "tensor"),
            P(),
            P(None, "tensor"),
            P(("dp", "fsdp"), "tensor", None),
        ),
        out_specs=(
            P(("dp", "fsdp"), "tensor", None),
            P(),
            P(None, "tensor"),
            P(),
            P(None, "tensor"),
        ),
        check_vma=False,
    )
```

profile of v0, /device:TPU:0, one launch (start us, length us, event | category | flops | bytes accessed | tf_op | source)
XLA Modules:
  0.0 610.3 jit_solution(15705203789652585321)
XLA Ops:
  7.9 2.8 fusion.1
  12.4 5.3 collective-permute-start
  19.0 65.8 %collective-permute-done = bf16[192,8192]{1,0:T(8,128)(2,1)S(1)} collective-permute-done((bf16[192,8192]{1,0:T(8,128)(2,1)S(1)}, bf16[192,8192]{1,0:T(8,128)(2,1)S(1)}, u32[]{:S(2)}, u32[]{:S(2)}) %collective-permute-start) | collective-permute-done | bytes 3145760 | tf_op jit(solution)/shard_map/ppermute | solution.py:176
  85.7 3.5 collective-permute-done.2
  93.9 68.0 %collective-permute-done.3 = bf16[192,8192]{1,0:T(8,128)(2,1)} collective-permute-done((bf16[192,8192]{1,0:T(8,128)(2,1)S(1)}, bf16[192,8192]{1,0:T(8,128)(2,1)}, u32[]{:S(2)}, u32[]{:S(2)}) %collective-permute-start.3) | collective-permute-done | bytes 3145760 | tf_op jit(solution)/shard_map/ppermute | solution.py:177
  164.2 2.9 all_to_all.26
  168.7 3.6 all-to-all-start
  172.3 3.0 fusion.4
  175.3 85.9 %all-gather = bf16[4,192,32]{1,2,0:T(8,128)(2,1)S(1)} all-gather(bf16[1,192,32]{1,2,0:T(8,128)(2,1)S(1)} %fusion.4), channel_id=1, replica_groups=mesh['dp'=4,'fsdp'=2,'tensor'=4] {'tensor'}, dimensions={0}, use_global_device_ids=true | all-gather | bytes 61440 | tf_op jit(solution)/shard_map/all_gather | solution.py:168
  265.0 10.5 %convolution_dynamic-update-slice_fusion.6 = f32[1344,1280]{1,0:T(8,128)S(1)} fusion(bf16[192,8192]{1,0:T(8,128)(2,1)} %collective-permute-done.4, bf16[8192,1280]{1,0:T(8,128)(2,1)} %all-gather.3.cloned.1.call-done), kind=kOutput, calls=%fused_computation.13 | convolution fusion | flops 4026531840 | bytes 25100288 | tf_op jit(solution)/shard_map/dot_general | solution.py:181
  275.5 9.4 %convolution_dynamic-update-slice_fusion.5 = f32[1344,1280]{1,0:T(8,128)S(1)} fusion(f32[1344,1280]{1,0:T(8,128)S(1)} %convolution_dynamic-update-slice_fusion.6, bf16[192,8192]{1,0:T(8,128)(2,1)S(1)} %copy-done.12, bf16[8192,1280]{1,0:T(8,128)(2,1)} %all-gather.3.cloned.1.call-done), kind=kOutput, calls=%fused_computation.12 | convolution fusion | flops 4026531840 | bytes 25100288 | tf_op jit(solution)/shard_map/dot_general | solution.py:181
  284.9 9.4 %convolution_dynamic-update-slice_fusion.4 = f32[1344,1280]{1,0:T(8,128)S(1)} fusion(f32[1344,1280]{1,0:T(8,128)S(1)} %convolution_dynamic-update-slice_fusion.5, bf16[192,8192]{1,0:T(8,128)(2,1)S(1)} %copy-done.10, bf16[8192,1280]{1,0:T(8,128)(2,1)} %all-gather.3.cloned.1.call-done), kind=kOutput, calls=%fused_computation.11 | convolution fusion | flops 4026531840 | bytes 25100288 | tf_op jit(solution)/shard_map/dot_general | solution.py:181
  294.3 9.4 %convolution_dynamic-update-slice_fusion.3 = f32[1344,1280]{1,0:T(8,128)S(1)} fusion(f32[1344,1280]{1,0:T(8,128)S(1)} %convolution_dynamic-update-slice_fusion.4, bf16[192,8192]{1,0:T(8,128)(2,1)S(1)} %copy-done.3, bf16[8192,1280]{1,0:T(8,128)(2,1)} %all-gather.3.cloned.1.call-done), kind=kOutput, calls=%fused_computation.10 | convolution fusion | flops 4026531840 | bytes 25100288 | tf_op jit(solution)/shard_map/dot_general | solution.py:181
  303.7 9.2 %convolution_dynamic-update-slice_fusion.2 = f32[1344,1280]{1,0:T(8,128)S(1)} fusion(f32[1344,1280]{1,0:T(8,128)S(1)} %convolution_dynamic-update-slice_fusion.3, bf16[192,8192]{1,0:T(8,128)(2,1)S(1)} %copy-done.8, bf16[8192,1280]{1,0:T(8,128)(2,1)} %all-gather.3.cloned.1.call-done), kind=kOutput, calls=%fused_computation.9 | convolution fusion | flops 4026531840 | bytes 25100288 | tf_op jit(solution)/shard_map/dot_general | solution.py:181
  313.0 10.7 %convolution_dynamic-update-slice_fusion.1 = f32[1344,1280]{1,0:T(8,128)S(1)} fusion(f32[1344,1280]{1,0:T(8,128)S(1)} %convolution_dynamic-update-slice_fusion.2, bf16[192,8192]{1,0:T(8,128)(2,1)} %collective-permute-done.3, bf16[8192,1280]{1,0:T(8,128)(2,1)} %all-gather.3.cloned.1.call-done), kind=kOutput, calls=%fused_computation.8 | convolution fusion | flops 4026531840 | bytes 25100288 | tf_op jit(solution)/shard_map/dot_general | solution.py:181
  323.7 7.6 %collective-permute-done.5 = bf16[192,8192]{1,0:T(8,128)(2,1)S(1)} collective-permute-done((bf16[192,8192]{1,0:T(8,128)(2,1)}, bf16[192,8192]{1,0:T(8,128)(2,1)S(1)}, u32[]{:S(2)}, u32[]{:S(2)}) %collective-permute-start.5) | collective-permute-done | bytes 3145760 | tf_op jit(solution)/shard_map/ppermute | solution.py:177
  331.4 9.2 %convolution_dynamic-update-slice_fusion = f32[1344,1280]{1,0:T(8,128)S(1)} fusion(f32[1344,1280]{1,0:T(8,128)S(1)} %convolution_dynamic-update-slice_fusion.1, bf16[192,8192]{1,0:T(8,128)(2,1)S(1)} %collective-permute-done.5, bf16[8192,1280]{1,0:T(8,128)(2,1)} %all-gather.3.cloned.1.call-done), kind=kOutput, calls=%fused_computation.7 | convolution fusion | flops 4026531840 | bytes 25100288 | tf_op jit(solution)/shard_map/dot_general | solution.py:181
  343.5 31.0 %attention.1 = (bf16[768,1024]{1,0:T(8,128)(2,1)}, f32[16,1024]{1,0:T(8,128)}, f32[16,128]{1,0:T(8,128)S(1)}, f32[768,16]{1,0:T(8,128)S(1)}, f32[768,16]{1,0:T(8,128)S(1)}) custom-call(f32[768,1280]{1,0:T(8,128)} %constant_dynamic-slice_fusion.q_ref.k_ref.v_ref, f32[768,1280]{1,0:T(8,128)} %constant_dynamic-slice_fusion.q_ref.k_ref.v_ref, ...), custom_call_target="tpu_custom_call" | custom-call | flops 6039797760 | bytes 7077888 | tf_op jit(solution)/shard_map/attention/pallas_call | solution.py:111
  375.8 19.1 %reduce-scatter.4.cloned.1.call-done = f32[192,32]{1,0:T(8,128)} async-done(((f32[768,32]{1,0:T(8,128)}), f32[192,32]{1,0:T(8,128)}) %reduce-scatter.4.cloned.1.call-update) | async-done | bytes 24592
  395.8 3.6 fusion
  399.5 3.6 all-to-all-start.1
  403.6 14.8 %psum.23 = f32[16,128]{1,0:T(8,128)} all-reduce(f32[16,128]{1,0:T(8,128)S(1)} %get-tuple-element.20), channel_id=1, replica_groups=mesh['dp'=4,'fsdp'=2,'tensor'=4] {'dp','fsdp'}, use_global_device_ids=true, to_apply=%region_4.0 | all-reduce | flops 2048 | bytes 16384 | tf_op jit(solution)/shard_map/psum | solution.py:198
  418.4 128.2 %all-reduce.3.cloned.1.call-done = f32[8192,32]{0,1:T(8,128)} async-done(((f32[8192,32]{0,1:T(8,128)}), f32[8192,32]{0,1:T(8,128)}) %all-reduce.3.cloned.1.call-update) | async-done | bytes 1048592 | tf_op jit(solution)/shard_map/psum | solution.py:197
  552.5 49.8 %all-reduce.5.cloned.1.call-done = f32[16,1024]{1,0:T(8,128)} async-done(((f32[16,1024]{1,0:T(8,128)}), f32[16,1024]{1,0:T(8,128)}) %all-reduce.5.cloned.1.call-update) | async-done | bytes 65552 | tf_op jit(solution)/shard_map/psum | solution.py:198
  (62 shorter events, 30.0 us)
Async XLA Ops:
  7.2 3.6 copy-start.4
  7.2 154.7 %all-gather.3.cloned.1.call-start = ((), (), s32[]{:S(2)}) async-start(), calls=%async_computation.3 | async-start | bytes 23592960 | tf_op jit(solution)/shard_map/all_gather | solution.py:163
  12.4 5.3 copy-start.2
  12.4 159.9 %copy-start.5 = (bf16[8192,16]{0,1:T(8,128)(2,1)S(1)}, bf16[8192,16]{0,1:T(8,128)(2,1)}, u32[]{:S(2)}) copy-start(bf16[8192,16]{0,1:T(8,128)(2,1)} %param.13) | copy-start | bytes 786436
  12.4 159.9 %copy-start.6 = (bf16[8192,16]{0,1:T(8,128)(2,1)S(1)}, bf16[8192,16]{0,1:T(8,128)(2,1)}, u32[]{:S(2)}) copy-start(bf16[8192,16]{0,1:T(8,128)(2,1)} %param.11) | copy-start | bytes 786436
  12.4 72.4 %collective-permute-start = (bf16[192,8192]{1,0:T(8,128)(2,1)S(1)}, bf16[192,8192]{1,0:T(8,128)(2,1)S(1)}, u32[]{:S(2)}, u32[]{:S(2)}) collective-permute-start(bf16[192,8192]{1,0:T(8,128)(2,1)S(1)} %fusion.3), channel_id=1, source_target_pairs={{0,1},{1,2},{2,3},{4,5},{5,6},{6,7},{8,9},{9,10},{10,11},{12,13},{... | collective-permute-start | bytes 9437192 | tf_op jit(solution)/shard_map/ppermute | solution.py:176
  17.7 71.5 %collective-permute-start.2 = (bf16[192,8192]{1,0:T(8,128)(2,1)S(1)}, bf16[192,8192]{1,0:T(8,128)(2,1)S(1)}, u32[]{:S(2)}, u32[]{:S(2)}) collective-permute-start(bf16[192,8192]{1,0:T(8,128)(2,1)S(1)} %fusion.3), channel_id=1, source_target_pairs={{1,0},{2,1},{3,2},{5,4},{6,5},{7,6},{9,8},{10,9},{11,10},{13,12},{... | collective-permute-start | bytes 9437192 | tf_op jit(solution)/shard_map/ppermute | solution.py:177
  84.8 7.4 %copy-start.9 = (bf16[192,8192]{1,0:T(8,128)(2,1)}, bf16[192,8192]{1,0:T(8,128)(2,1)S(1)}, u32[]{:S(2)}) copy-start(bf16[192,8192]{1,0:T(8,128)(2,1)S(1)} %collective-permute-done) | copy-start | bytes 9437188
  84.8 7.4 %collective-permute-start.1 = (bf16[192,8192]{1,0:T(8,128)(2,1)S(1)}, bf16[192,8192]{1,0:T(8,128)(2,1)S(1)}, u32[]{:S(2)}, u32[]{:S(2)}) collective-permute-start(bf16[192,8192]{1,0:T(8,128)(2,1)S(1)} %collective-permute-done), channel_id=1, source_target_pairs={{1,2},{2,3},{5,6},{6,7},{9,10},{10,11},{13,14},{14,15},{17,18},{18... | collective-permute-start | bytes 9437192 | tf_op jit(solution)/shard_map/ppermute | solution.py:176
  89.1 1.8 copy-start.7
  90.9 70.9 %collective-permute-start.3 = (bf16[192,8192]{1,0:T(8,128)(2,1)S(1)}, bf16[192,8192]{1,0:T(8,128)(2,1)}, u32[]{:S(2)}, u32[]{:S(2)}) collective-permute-start(bf16[192,8192]{1,0:T(8,128)(2,1)S(1)} %collective-permute-done.2), channel_id=1, source_target_pairs={{1,0},{2,1},{5,4},{6,5},{9,8},{10,9},{13,12},{14,13},{17,16},{18,1... | collective-permute-start | bytes 9437192 | tf_op jit(solution)/shard_map/ppermute | solution.py:177
  92.2 1.6 copy-start.11
  161.8 103.1 %collective-permute-start.4 = (bf16[192,8192]{1,0:T(8,128)(2,1)}, bf16[192,8192]{1,0:T(8,128)(2,1)}, u32[]{:S(2)}, u32[]{:S(2)}) collective-permute-start(bf16[192,8192]{1,0:T(8,128)(2,1)} %copy-done.11), channel_id=1, source_target_pairs={{2,3},{6,7},{10,11},{14,15},{18,19},{22,23},{26,27},{30,31}} | collective-permute-start | bytes 9437192 | tf_op jit(solution)/shard_map/ppermute | solution.py:176
  168.7 174.1 %all-to-all-start = ((bf16[192,4,1024]{2,0,1:T(8,128)(2,1)}), bf16[192,4,1024]{2,0,1:T(8,128)(2,1)S(1)}, u32[]{:S(2)}, u32[]{:S(2)}) async-start(bf16[192,4,1024]{2,0,1:T(8,128)(2,1)} %copy.22), calls=%async_computation | async-start | bytes 3145728 | tf_op jit(solution)/shard_map/all_to_all | solution.py:165
  172.2 222.6 %reduce-scatter.4.cloned.1.call-start = ((), (), s32[]{:S(2)}) async-start(), calls=%async_computation.6 | async-start | bytes 491520
  263.2 12.3 %copy-start.12 = (bf16[192,8192]{1,0:T(8,128)(2,1)S(1)}, bf16[192,8192]{1,0:T(8,128)(2,1)}, u32[]{:S(2)}) copy-start(bf16[192,8192]{1,0:T(8,128)(2,1)} %copy-done.11) | copy-start | bytes 9437188
  263.2 68.1 %collective-permute-start.5 = (bf16[192,8192]{1,0:T(8,128)(2,1)}, bf16[192,8192]{1,0:T(8,128)(2,1)S(1)}, u32[]{:S(2)}, u32[]{:S(2)}) collective-permute-start(bf16[192,8192]{1,0:T(8,128)(2,1)} %collective-permute-done.3), channel_id=1, source_target_pairs={{1,0},{5,4},{9,8},{13,12},{17,16},{21,20},{25,24},{29,28}} | collective-permute-start | bytes 9437192 | tf_op jit(solution)/shard_map/ppermute | solution.py:177
  275.5 9.4 %copy-start.10 = (bf16[192,8192]{1,0:T(8,128)(2,1)S(1)}, bf16[192,8192]{1,0:T(8,128)(2,1)}, u32[]{:S(2)}) copy-start(bf16[192,8192]{1,0:T(8,128)(2,1)} %copy-done.9) | copy-start | bytes 9437188
  284.9 9.4 %copy-start.3 = (bf16[192,8192]{1,0:T(8,128)(2,1)S(1)}, bf16[192,8192]{1,0:T(8,128)(2,1)}, u32[]{:S(2)}) copy-start(bf16[192,8192]{1,0:T(8,128)(2,1)} %copy-done.2) | copy-start | bytes 9437188
  294.3 9.4 %copy-start.8 = (bf16[192,8192]{1,0:T(8,128)(2,1)S(1)}, bf16[192,8192]{1,0:T(8,128)(2,1)}, u32[]{:S(2)}) copy-start(bf16[192,8192]{1,0:T(8,128)(2,1)} %copy-done.7) | copy-start | bytes 9437188
  340.6 2.1 copy-start.1
  375.7 170.9 %all-reduce.3.cloned.1.call-start = ((), (), s32[]{:S(2)}) async-start(), calls=%async_computation.4 | async-start | bytes 2097152 | tf_op jit(solution)/shard_map/psum | solution.py:197
  399.5 149.4 %all-to-all-start.1 = ((bf16[4,192,1024]{2,1,0:T(8,128)(2,1)}), bf16[4,192,1024]{2,1,0:T(8,128)(2,1)S(1)}, u32[]{:S(2)}, u32[]{:S(2)}) async-start(bf16[4,192,1024]{2,1,0:T(8,128)(2,1)} %bitcast.6), calls=%async_computation.1 | async-start | bytes 3145728 | tf_op jit(solution)/shard_map/all_to_all | solution.py:190
  403.0 199.2 %all-reduce.5.cloned.1.call-start = ((), (), s32[]{:S(2)}) async-start(), calls=%async_computation.5 | async-start | bytes 131072 | tf_op jit(solution)/shard_map/psum | solution.py:198
  (1 other events, 0.8 us)
Sparse Core Ops, SparseCore 0:
  9.9 110.1 all-gather.2
  375.8 18.9 reduce-scatter.3
  400.1 146.5 all-reduce.2
  550.1 52.1 all-reduce.4
where the time goes:
time: 611 us; the launch traced here: 610 us
  waiting for transfers between devices  343 us (56%)
  blocking collectives  101 us (17%)
  matrix products  74.4 us (12%)
  Pallas kernels  31 us (5%)
  local copies, waits for them, and re-layouts  20.6 us (3%)
  starting transfers between devices  20.1 us (3%)
  between operations  14.1 us (2%)
  other arithmetic  6.2 us (1%)
    psum x1, waiting for transfers between devices, local(): down_gradient = lax.psum(down_gradient, ('dp', 'fsdp', 'tensor')).T  128 us
    all_gather x1, blocking collectives, local(): down_projected = lax.all_gather(down_own, 'tensor', axis=0, tiled=True)  85.9 us
    ppermute x3, waiting for transfers between devices, local(): lax.ppermute(down_block, 'tensor', [(i, i - 1) for i in range(1, count -...  79.1 us
    dot_general x7, matrix products, local(): jnp.dot(rows, weights, preferred_element_type=jnp.float32)  67.9 us
    ppermute x3, waiting for transfers between devices, local(): lax.ppermute(up_block, 'tensor', [(i, i + 1) for i in range(step - 1, cou...  65.8 us
    psum x1, waiting for transfers between devices, local(): lax.psum((query_up_gradient, value_up_gradient), ('dp', 'fsdp'))  49.8 us
    pallas_call x1, Pallas kernels, attention(): pl.pallas_call(functools.partial(attention_kernel, block), grid=(groups,...  31 us
    unnamed x5, waiting for transfers between devices  20.3 us
  transfers between devices with their start and end apart: 12, of which 7 were waited for; matrix products, arithmetic and copies ran while one was open for 14% of the time, Pallas kernels for 0%

commit v1 on v0

v1 whole, which is shorter than its diff:
```python
import functools
import math

import jax
import jax.numpy as jnp
from jax import lax
from jax.experimental import pallas as pl
from jax.experimental.pallas import tpu as pltpu
from jax.sharding import PartitionSpec as P

HD = 128
QUERY_PER_KV = 8
LANES = 128
CORES = 2
PIECES = 4

EPSILON = 1e-05
ADAPTER_SCALE = 2.0
ROPE_BASE = 500000.0
MESH = pl.DeviceIdType.MESH


def normalize(own_rows, norm_gain):
    widened = own_rows.astype(jnp.float32)
    mean_square = jnp.mean(widened * widened, axis=-1, keepdims=True)
    return (widened * lax.rsqrt(mean_square + EPSILON) * norm_gain).astype(jnp.bfloat16)


def rotary_tables(sequence_length):
    half_dim = HD // 2
    positions = jnp.arange(sequence_length, dtype=jnp.float32)[:, None]
    inv_freq = ROPE_BASE ** (-jnp.arange(half_dim, dtype=jnp.float32) / half_dim)
    angles = positions * inv_freq
    cosine, sine = jnp.cos(angles), jnp.sin(angles)
    return jnp.concatenate([cosine, cosine], 1), jnp.concatenate([-sine, sine], 1)


def dot(a, b, dims):
    return lax.dot_general(a, b, (dims, ((), ())), preferred_element_type=jnp.float32)


class Place:
    def __init__(self, n, chips, fsdp):
        self.n, self.chips, self.fsdp = n, chips, fsdp
        dp = lax.axis_index("dp")
        self.x, self.c = dp // CORES, lax.rem(dp, CORES)
        self.y, self.z = lax.axis_index("fsdp"), lax.axis_index("tensor")

    def chip(self, a, e):
        return lax.rem(self.x + a, self.chips), lax.rem(self.y + e, self.fsdp)

    def shard(self, a, e, b):
        x, y = self.chip(a, e)
        core = self.c if b == 0 else 1 - self.c
        return (x * CORES + core) * self.fsdp + y

    def plane(self, a, e):
        x, y = self.chip(a, e)
        return x * self.fsdp + y

    def at(self, a, e):
        x, y = self.chip(a, e)
        return {"dp": x * CORES + self.c, "fsdp": y}

    def partner(self):
        return {"dp": self.x * CORES + 1 - self.c}

    def line(self, step):
        return {"tensor": lax.rem(self.z + step, self.n)}

    def others(self):
        return [(a, e) for a in range(self.chips) for e in range(self.fsdp) if (a, e) != (0, 0)]


def remote(src, dst, send, recv, device):
    return pltpu.make_async_remote_copy(
        src_ref=src, dst_ref=dst, send_sem=send, recv_sem=recv, device_id=device, device_id_type=MESH
    )


def greet(devices):
    barrier = pltpu.get_barrier_semaphore()
    for device in devices:
        pl.semaphore_signal(barrier, inc=1, device_id=device, device_id_type=MESH)
    pl.semaphore_wait(barrier, len(devices))


def project_kernel(
    n, chips, fsdp, tok_ref, w_ref, adp_ref, g_ref,
    proj_ref, down_ref, grad_ref,
    wide, blocks, down_sum,
    local_sem, tok_send, tok_recv, g_send, g_recv,
    a1, a2, b1, b2, cross, w_recv,
):
    me = Place(n, chips, fsdp)
    z = me.z
    rows, depth = tok_ref.shape
    shard_rows, cols = w_ref.shape
    half = shard_rows // 2
    span = depth // PIECES
    g_cols = grad_ref.shape[1]

    greet(
        [me.line(s) for s in range(1, n)]
        + [me.at(a, 0) for a in range(1, chips)]
        + [me.at(0, e) for e in range(1, fsdp)]
        + [me.partner()]
    )

    def columns(p):
        return pl.ds(pl.multiple_of(p * span, LANES), span)

    def token_copy(block, p, up, own):
        source = tok_ref.at[:, columns(p)] if own else blocks.at[block, :, columns(p)]
        return remote(
            source, blocks.at[block, :, columns(p)],
            tok_send.at[0 if up else 1, block, p], tok_recv.at[block, p],
            {"tensor": jnp.where(up, jnp.minimum(z + 1, n - 1), jnp.maximum(z - 1, 0))},
        )

    def w_rows(shard, h):
        return pl.ds(pl.multiple_of(shard * shard_rows + h * half, half), half)

    def w_copy(a, e, h, target, sem, own):
        shard = me.shard(a, e, 0)
        place = wide.at[w_rows(shard, h)]
        return remote(
            w_ref.at[pl.ds(h * half, half)] if own else place, place, sem, w_recv.at[shard, h], target
        )

    def w_wait(a, e, b, h):
        shard = me.shard(a, e, b)
        place = wide.at[w_rows(shard, h)]
        remote(place, place, cross.at[0, 0, 0], w_recv.at[shard, h], me.partner()).wait_recv()

    up_ok, down_ok = z < n - 1, z > 0
    for p in range(PIECES):
        @pl.when(up_ok)
        def _():
            token_copy(z, p, True, True).start()

        @pl.when(down_ok)
        def _():
            token_copy(z, p, False, True).start()
    own_w = pltpu.make_async_copy(
        w_ref, wide.at[pl.ds(pl.multiple_of(me.shard(0, 0, 0) * shard_rows, shard_rows), shard_rows)],
        local_sem.at[0],
    )
    own_t = pltpu.make_async_copy(tok_ref, blocks.at[z], local_sem.at[1])
    first_a = [w_copy(0, 0, 0, me.at(0, e), a1.at[e], True) for e in range(1, fsdp)]
    first_b = [w_copy(0, 0, 1, me.at(a, 0), b1.at[a], True) for a in range(1, chips)]
    next_a = [w_copy(0, 0, 0, me.at(a, 0), a2.at[a, 0], True) for a in range(1, chips)]
    next_b = [w_copy(0, 0, 1, me.at(0, e), b2.at[0, e], True) for e in range(1, fsdp)]
    own_cross = [w_copy(0, 0, h, me.partner(), cross.at[0, 0, h], True) for h in range(2)]
    w_sent = first_a + first_b + next_a + next_b + own_cross
    for copy in w_sent:
        copy.start()
    own_t.start()
    own_w.start()

    proj_ref[...] = jnp.zeros_like(proj_ref)
    down_sum[...] = jnp.zeros_like(down_sum)

    grads = []
    for s in range(1, n):
        to = lax.rem(z + s, n)
        grads.append(remote(
            g_ref.at[:, pl.ds(pl.multiple_of(to * g_cols, g_cols), g_cols)],
            grad_ref.at[pl.ds(pl.multiple_of(z * rows, rows), rows)],
            g_send.at[s], g_recv.at[s], me.line(s),
        ))
    for copy in grads:
        copy.start()
    own_g = pltpu.make_async_copy(
        g_ref.at[:, pl.ds(pl.multiple_of(z * g_cols, g_cols), g_cols)],
        grad_ref.at[pl.ds(pl.multiple_of(z * rows, rows), rows)], local_sem.at[2],
    )
    own_g.start()

    def pass_on(copies):
        for copy in copies:
            copy.start()
            w_sent.append(copy)

    for e in range(1, fsdp):
        w_wait(0, e, 0, 0)
        pass_on([w_copy(0, e, 0, me.at(a, 0), a2.at[a, e], False) for a in range(1, chips)])
        pass_on([w_copy(0, e, 0, me.partner(), cross.at[0, e, 0], False)])
    for a in range(1, chips):
        w_wait(a, 0, 0, 1)
        pass_on([w_copy(a, 0, 1, me.at(0, e), b2.at[a, e], False) for e in range(1, fsdp)])
        pass_on([w_copy(a, 0, 1, me.partner(), cross.at[a, 0, 1], False)])
    for a in range(1, chips):
        w_wait(a, 0, 0, 0)
        pass_on([w_copy(a, 0, 0, me.partner(), cross.at[a, 0, 0], False)])
    for e in range(1, fsdp):
        w_wait(0, e, 0, 1)
        pass_on([w_copy(0, e, 1, me.partner(), cross.at[0, e, 1], False)])

    def arrive(block, p, up):
        token_copy(block, p, up, False).wait_recv()

        @pl.when(up_ok if up else down_ok)
        def _():
            token_copy(block, p, up, False).start()

    def arrive_both(s, p):
        @pl.when(z - s >= 0)
        def _():
            arrive(jnp.maximum(z - s, 0), p, True)

        @pl.when(z + s <= n - 1)
        def _():
            arrive(jnp.minimum(z + s, n - 1), p, False)

    width = 2 * LANES

    def multiply(block, p):
        at_rows = pl.ds(pl.multiple_of(block * rows, rows), rows)
        deep = pl.ds(pl.multiple_of(p * span, span), span)

        @pl.loop(0, cols // width)
        def _(tile):
            lanes = pl.ds(pl.multiple_of(tile * width, width), width)
            proj_ref[at_rows, lanes] += dot(blocks[block, :, columns(p)], wide[deep, lanes], ((1,), (0,)))

        down_sum[at_rows, :] += dot(blocks[block, :, columns(p)], adp_ref[deep, :], ((1,), (0,)))

    for p in range(PIECES):
        arrive_both(1, p)
    for a in range(1, chips):
        for e in range(1, fsdp):
            for h in range(2):
                w_wait(a, e, 0, h)
                pass_on([w_copy(a, e, h, me.partner(), cross.at[a, e, h], False)])
    for a in range(chips):
        for e in range(fsdp):
            for h in range(2):
                w_wait(a, e, 1, h)
    own_w.wait()
    own_t.wait()

    @pl.loop(0, PIECES)
    def _(p):
        multiply(z, p)

    for s in range(1, n):
        @pl.loop(0, PIECES)
        def _(p):
            @pl.when(z - s >= 0)
            def _():
                multiply(jnp.maximum(z - s, 0), p)

            @pl.when(z + s <= n - 1)
            def _():
                multiply(jnp.minimum(z + s, n - 1), p)

            if s + 1 < n:
                arrive_both(s + 1, p)

    down_ref[...] = down_sum[...].astype(jnp.bfloat16)

    own_g.wait()
    for copy in grads:
        copy.wait()
    for copy in w_sent:
        copy.wait_send()

    @pl.loop(0, PIECES)
    def _(p):
        @pl.when(up_ok)
        def _():
            token_copy(z, p, True, True).wait_send()

        @pl.when(down_ok)
        def _():
            token_copy(z, p, False, True).wait_send()

        for s in range(1, n):
            @pl.when((z - s >= 0) & up_ok)
            def _():
                token_copy(jnp.maximum(z - s, 0), p, True, False).wait_send()

            @pl.when((z + s <= n - 1) & down_ok)
            def _():
                token_copy(jnp.minimum(z + s, n - 1), p, False, False).wait_send()


def project(sizes, own, w_qkv, adapters, out_grad):
    n, chips, fsdp = sizes
    rows, depth = own.shape
    shard_rows, cols = w_qkv.shape
    g_cols = out_grad.shape[1] // n
    shards = chips * CORES * fsdp
    dma = pltpu.SemaphoreType.DMA
    anywhere = pl.BlockSpec(memory_space=pl.ANY)
    vmem = pl.BlockSpec(memory_space=pltpu.VMEM)
    return pl.pallas_call(
        functools.partial(project_kernel, n, chips, fsdp),
        in_specs=[anywhere, anywhere, vmem, anywhere],
        out_specs=[vmem, vmem, anywhere],
        out_shape=[
            jax.ShapeDtypeStruct((n * rows, cols), jnp.float32),
            jax.ShapeDtypeStruct((n * rows, LANES), jnp.bfloat16),
            jax.ShapeDtypeStruct((n * rows, g_cols), jnp.bfloat16),
        ],
        scratch_shapes=[
            pltpu.VMEM((depth, cols), jnp.bfloat16),
            pltpu.VMEM((n, rows, depth), jnp.bfloat16),
            pltpu.VMEM((n * rows, LANES), jnp.float32),
            dma((3,)),
            dma((2, n, PIECES)),
            dma((n, PIECES)),
            dma((n,)),
            dma((n,)),
            dma((fsdp,)),
            dma((chips, fsdp)),
            dma((chips,)),
            dma((chips, fsdp)),
            dma((chips, fsdp, 2)),
            dma((shards, 2)),
        ],
        compiler_params=pltpu.CompilerParams(
            collective_id=0, has_side_effects=True, vmem_limit_bytes=60 * 2**20
        ),
        cost_estimate=pl.CostEstimate(
            flops=2 * n * rows * depth * cols, bytes_accessed=depth * cols * 2, transcendentals=0
        ),
        name="project",
    )(own, w_qkv, adapters, out_grad)


def attention_kernel(
    block, n, q_ref, k_ref, v_ref, dq_ref, dv_ref, qup_ref, vup_ref, cos_ref, sin_ref, g_ref,
    out_ref, gbq_ref, gbv_ref, mid_ref,
    keys, values, value_grad, query_grad, staged, send_sem, recv_sem, local_sem,
):
    group, head = pl.program_id(0), pl.program_id(1)
    groups, heads = pl.num_programs(0), pl.num_programs(1)
    length = q_ref.shape[0]
    rows_each = length // n
    rank = qup_ref.shape[0]
    scale = 1.0 / math.sqrt(HD)
    z = lax.axis_index("tensor")
    index = group * heads + head

    @pl.when(index == 0)
    def _():
        greet([{"tensor": lax.rem(z + s, n)} for s in range(1, n)])
        mid_ref[...] = jnp.zeros_like(mid_ref)

    @pl.when(head == 0)
    def _():
        k = k_ref[...].astype(jnp.bfloat16).astype(jnp.float32)
        keys[...] = (k * cos_ref[...] + pltpu.roll(k, HD // 2, 1) * sin_ref[...]).astype(jnp.bfloat16)
        values[...] = (
            v_ref[...] + ADAPTER_SCALE * dot(dv_ref[...], vup_ref[...], ((1,), (0,)))
        ).astype(jnp.bfloat16)
        value_grad[...] = jnp.zeros_like(value_grad)

    for start in range(0, length, block):
        rows = pl.ds(start, block)
        reach = start + block
        q = (
            q_ref[rows, :] + ADAPTER_SCALE * dot(dq_ref[rows, :], qup_ref[...], ((1,), (0,)))
        ).astype(jnp.bfloat16).astype(jnp.float32)
        cosine, sine = cos_ref[rows, :], sin_ref[rows, :]
        turned = (q * cosine + pltpu.roll(q, HD // 2, 1) * sine).astype(jnp.bfloat16)
        k, v, g = keys[pl.ds(0, reach), :], values[pl.ds(0, reach), :], g_ref[rows, :]
        scores = dot(turned, k, ((1,), (1,))) * scale
        row = lax.broadcasted_iota(jnp.int32, scores.shape, 0) + start
        col = lax.broadcasted_iota(jnp.int32, scores.shape, 1)
        scores = jnp.where(row >= col, scores, -1e30)
        weights = jnp.exp(scores - jnp.max(scores, axis=-1, keepdims=True))
        wide = weights * (1.0 / jnp.sum(weights, axis=-1, keepdims=True))
        probabilities = wide.astype(jnp.bfloat16)
        staged[index, rows, :] = dot(probabilities, v, ((1,), (0,))).astype(jnp.bfloat16)
        value_grad[pl.ds(0, reach), :] += dot(probabilities, g, ((0,), (0,)))
        prob_grad = dot(g, v, ((1,), (1,)))
        inner = jnp.sum(prob_grad * wide, axis=-1, keepdims=True)
        score_grad = (wide * (prob_grad - inner) * scale).astype(jnp.bfloat16)
        turned_grad = dot(score_grad, k, ((1,), (0,))).astype(jnp.bfloat16).astype(jnp.float32)
        query_grad[rows, :] = (
            turned_grad * cosine - pltpu.roll(turned_grad, HD // 2, 1) * sine
        ).astype(jnp.bfloat16)

    gq = query_grad[...]
    gbq_ref[...] = ADAPTER_SCALE * dot(dq_ref[...], gq, ((0,), (0,)))
    mid_ref[:, pl.ds(0, rank)] += dot(gq, qup_ref[...], ((1,), (1,)))

    @pl.when(head == heads - 1)
    def _():
        gv = value_grad[...].astype(jnp.bfloat16)
        gbv_ref[...] = ADAPTER_SCALE * dot(dv_ref[...], gv, ((0,), (0,)))
        mid_ref[:, pl.ds(rank, rank)] += dot(gv, vup_ref[...], ((1,), (1,)))

    def columns(which, owner):
        return pl.ds(pl.multiple_of((owner * groups * heads + which) * HD, HD), HD)

    def copies(which):
        found = []
        for s in range(1, n):
            to = lax.rem(z + s, n)
            found.append(remote(
                staged.at[which, pl.ds(pl.multiple_of(to * rows_each, rows_each), rows_each)],
                out_ref.at[:, columns(which, z)],
                send_sem.at[s, which], recv_sem.at[s, which], {"tensor": to},
            ))
        mine = pltpu.make_async_copy(
            staged.at[which, pl.ds(pl.multiple_of(z * rows_each, rows_each), rows_each)],
            out_ref.at[:, columns(which, z)], local_sem.at[which],
        )
        return found, mine

    found, mine = copies(index)
    for copy in found:
        copy.start()
    mine.start()

    @pl.when(index == groups * heads - 1)
    def _():
        @pl.loop(0, groups * heads)
        def _(which):
            found, mine = copies(which)
            for copy in found:
                copy.wait()
            mine.wait()


def attention(n, projected, down_q, down_v, query_up, value_up, grad_rows):
    length, cols = projected.shape
    rank = down_q.shape[1]
    per = QUERY_PER_KV + 2
    groups = cols // (per * HD)
    block = 256 if length % 256 == 0 else length
    cosine, sine = rotary_tables(length)
    heads = groups * QUERY_PER_KV
    whole = lambda shape: pl.BlockSpec(shape, lambda g, h: (0, 0))
    column = lambda n, index: pl.BlockSpec((n, HD), lambda g, h: (0, index(g, h)))
    by_head = lambda g, h: g * QUERY_PER_KV + h
    return pl.pallas_call(
        functools.partial(attention_kernel, block, n),
        grid=(groups, QUERY_PER_KV),
        in_specs=[
            column(length, lambda g, h: g * per + h),
            column(length, lambda g, h: g * per + QUERY_PER_KV),
            column(length, lambda g, h: g * per + QUERY_PER_KV + 1),
            whole((length, rank)),
            whole((length, rank)),
            column(rank, by_head),
            column(rank, lambda g, h: g),
            whole((length, HD)),
            whole((length, HD)),
            column(length, by_head),
        ],
        out_specs=[
            pl.BlockSpec(memory_space=pl.ANY),
            column(rank, by_head),
            column(rank, lambda g, h: g),
            whole((length, LANES)),
        ],
        out_shape=[
            jax.ShapeDtypeStruct((length // n, n * heads * HD), jnp.bfloat16),
            jax.ShapeDtypeStruct((rank, heads * HD), jnp.float32),
            jax.ShapeDtypeStruct((rank, groups * HD), jnp.float32),
            jax.ShapeDtypeStruct((length, LANES), jnp.float32),
        ],
        scratch_shapes=[
            pltpu.VMEM((length, HD), jnp.bfloat16),
            pltpu.VMEM((length, HD), jnp.bfloat16),
            pltpu.VMEM((length, HD), jnp.float32),
            pltpu.VMEM((length, HD), jnp.bfloat16),
            pltpu.VMEM((heads, length, HD), jnp.bfloat16),
            pltpu.SemaphoreType.DMA((n, heads)),
            pltpu.SemaphoreType.DMA((n, heads)),
            pltpu.SemaphoreType.DMA((heads,)),
        ],
        compiler_params=pltpu.CompilerParams(
            dimension_semantics=("arbitrary", "arbitrary"), vmem_limit_bytes=48 * 2**20,
            collective_id=1, has_side_effects=True,
        ),
        cost_estimate=pl.CostEstimate(
            flops=10 * heads * length * length * HD,
            bytes_accessed=length * cols * 4 + 2 * length * heads * HD * 2,
            transcendentals=heads * length * length,
        ),
        name="attention",
    )(projected, projected, projected, down_q, down_v, query_up, value_up, cosine, sine, grad_rows)


def finish_kernel(
    n, chips, fsdp, mid_ref, own_ref, gb_ref,
    down_ref, gbo_ref,
    mid_in, mid_own, part, part_in, spread, spread_in, line_sum, line_in, line_all, kept, other,
    gb_in, gb_all,
    mid_s, mid_r, core_s, core_r, plane_s, plane_r, line_s, line_r, all_s, all_r, keep_s, keep_r,
    gbp_s, gbp_r,
):
    me = Place(n, chips, fsdp)
    z, c = me.z, me.c
    rows, depth = own_ref.shape
    height = part.shape[1]
    count = chips * fsdp
    piece = spread.shape[2]
    tall = height // n
    gb_half = gb_ref.shape[0] // CORES
    here = me.plane(0, 0)
    others = me.others()
    greet([me.line(s) for s in range(1, n)] + [me.at(a, e) for a, e in others] + [me.partner()])

    def mid_rows(t):
        return pl.ds(pl.multiple_of(t * rows, rows), rows)

    def gb_rows(core):
        return pl.ds(pl.multiple_of(core * gb_half, gb_half), gb_half)

    def line_rows(t):
        return pl.ds(pl.multiple_of(t * tall, tall), tall)

    mids = [
        remote(mid_ref.at[mid_rows(lax.rem(z + s, n))], mid_in.at[s], mid_s.at[s], mid_r.at[s], me.line(s))
        for s in range(1, n)
    ]
    for copy in mids:
        copy.start()
    gb_core = remote(gb_ref.at[gb_rows(1 - c)], gb_in, core_s.at[1], core_r.at[1], me.partner())
    gb_core.start()

    total = mid_ref[mid_rows(z), :]
    for s, copy in zip(range(1, n), mids):
        copy.wait()
        total = total + mid_in[s]
    mid_own[...] = total.astype(jnp.bfloat16)

    width = 4 * LANES

    def product(core):
        @pl.loop(0, depth // 2 // width)
        def _(tile):
            lanes = pl.ds(pl.multiple_of(tile * width, width), width)
            source = pl.ds(pl.multiple_of(core * (depth // 2) + tile * width, width), width)
            whole = dot(mid_own[...], own_ref[:, source], ((0,), (0,)))
            part[core, :, lanes] = ADAPTER_SCALE * whole[:height]

    product(1 - c)
    core_copy = remote(part.at[1 - c], part_in, core_s.at[0], core_r.at[0], me.partner())
    core_copy.start()
    product(c)

    gb_core.wait()
    gb_all[here] = gb_ref[gb_rows(c), :] + gb_in[...]
    gb_plane = [
        remote(gb_all.at[here], gb_all.at[here], gbp_s.at[i], gbp_r.at[here], me.at(a, e))
        for i, (a, e) in enumerate(others)
    ]
    core_copy.wait()
    for k in range(count):
        lanes = pl.ds(k * piece, piece)
        summed = part[c, :, lanes] + part_in[:, lanes]
        part[c, :, lanes] = summed
        spread[k] = summed.astype(jnp.bfloat16)
    planes = []
    for i, (a, e) in enumerate(others):
        planes.append(remote(
            spread.at[me.plane(a, e)], spread_in.at[here], plane_s.at[i], plane_r.at[here], me.at(a, e)
        ))
        planes[-1].start()
    for copy in gb_plane:
        copy.start()

    def plane_wait(buffer, sems, a, e):
        source = me.plane(a, e)
        remote(buffer.at[source], buffer.at[source], plane_s.at[0], sems.at[source], me.at(a, e)).wait_recv()

    summed = part[c, :, pl.ds(pl.multiple_of(here * piece, piece), piece)]
    for a, e in others:
        plane_wait(spread_in, plane_r, a, e)
        summed = summed + spread_in[me.plane(a, e)].astype(jnp.float32)
    line_sum[...] = summed
    lines = [
        remote(line_sum.at[line_rows(lax.rem(z + s, n))], line_in.at[s], line_s.at[s], line_r.at[s], me.line(s))
        for s in range(1, n)
    ]
    for copy in lines:
        copy.start()
    summed = line_sum[line_rows(z), :]
    for s, copy in zip(range(1, n), lines):
        copy.wait_recv()
        summed = summed + line_in[s]
    line_all[line_rows(z), :] = summed
    alls = [
        remote(line_all.at[line_rows(z)], line_all.at[line_rows(z)], all_s.at[s], all_r.at[s], me.line(s))
        for s in range(1, n)
    ]
    for copy in alls:
        copy.start()

    for a, e in others:
        plane_wait(gb_all, gbp_r, a, e)
    gb_sum = gb_all[0]
    for k in range(1, count):
        gb_sum = gb_sum + gb_all[k]
    gbo_ref[gb_rows(c), :] = gb_sum
    gb_back = remote(gbo_ref.at[gb_rows(c)], gbo_ref.at[gb_rows(c)], core_s.at[2], core_r.at[2], me.partner())
    gb_back.start()

    for s in range(1, n):
        source = lax.rem(z + n - s, n)
        remote(
            line_all.at[line_rows(source)], line_all.at[line_rows(source)], all_s.at[s], all_r.at[s], me.line(s)
        ).wait_recv()
    kept[here] = line_all[...].astype(jnp.bfloat16)
    keeps = [
        remote(kept.at[here], kept.at[here], keep_s.at[i], keep_r.at[here], me.at(a, e))
        for i, (a, e) in enumerate(others)
    ]
    for copy in keeps:
        copy.start()
    for a, e in others:
        plane_wait(kept, keep_r, a, e)
    back = remote(kept, other, core_s.at[3], core_r.at[3], me.partner())
    back.start()

    def put(buffer, core):
        for k in range(count):
            start = pl.multiple_of(core * (depth // 2) + k * piece, piece)
            down_ref[:, pl.ds(start, piece)] = buffer[k].astype(jnp.float32)

    put(kept, c)
    back.wait()
    put(other, 1 - c)
    gb_back.wait_send()
    remote(
        gbo_ref.at[gb_rows(1 - c)], gbo_ref.at[gb_rows(1 - c)], core_s.at[2], core_r.at[2], me.partner()
    ).wait_recv()
    for copy in planes + gb_plane + lines + alls + keeps:
        copy.wait_send()


def finish(sizes, mid, own, gb, height):
    n, chips, fsdp = sizes
    rows, depth = own.shape
    count = chips * fsdp
    piece = depth // CORES // count
    dma = pltpu.SemaphoreType.DMA
    vmem = pl.BlockSpec(memory_space=pltpu.VMEM)
    f32, bf16 = jnp.float32, jnp.bfloat16
    return pl.pallas_call(
        functools.partial(finish_kernel, n, chips, fsdp),
        in_specs=[vmem] * 3,
        out_specs=[vmem] * 2,
        out_shape=[jax.ShapeDtypeStruct((height, depth), f32), jax.ShapeDtypeStruct(gb.shape, f32)],
        scratch_shapes=[
            pltpu.VMEM((n, rows, LANES), f32),
            pltpu.VMEM((rows, LANES), bf16),
            pltpu.VMEM((CORES, height, depth // CORES), f32),
            pltpu.VMEM((height, depth // CORES), f32),
            pltpu.VMEM((count, height, piece), bf16),
            pltpu.VMEM((count, height, piece), bf16),
            pltpu.VMEM((height, piece), f32),
            pltpu.VMEM((n, height // n, piece), f32),
            pltpu.VMEM((height, piece), f32),
            pltpu.VMEM((count, height, piece), bf16),
            pltpu.VMEM((count, height, piece), bf16),
            pltpu.VMEM((gb.shape[0] // CORES, gb.shape[1]), f32),
            pltpu.VMEM((count, gb.shape[0] // CORES, gb.shape[1]), f32),
            dma((n,)), dma((n,)),
            dma((4,)), dma((4,)),
            dma((count,)), dma((count,)),
            dma((n,)), dma((n,)),
            dma((n,)), dma((n,)),
            dma((count,)), dma((count,)),
            dma((count,)), dma((count,)),
        ],
        compiler_params=pltpu.CompilerParams(
            collective_id=2, has_side_effects=True, vmem_limit_bytes=32 * 2**20
        ),
        cost_estimate=pl.CostEstimate(
            flops=2 * rows * depth * LANES, bytes_accessed=rows * depth * 2, transcendentals=0
        ),
        name="finish",
    )(mid, own, gb)


def local(sizes, tokens, norm_gain, w_qkv, a_query, query_up_adapter, a_value, value_up_adapter, out_grad):
    n = sizes[0]
    own = normalize(tokens[0], norm_gain)
    rank = a_query.shape[1]
    depth = own.shape[1]
    adapters = jnp.concatenate(
        [a_query, a_value, jnp.zeros((depth, LANES - 2 * rank), a_query.dtype)], 1
    )
    projected, down_projected, grad_rows = project(sizes, own, w_qkv, adapters, out_grad[0])
    out_rows, query_up_gradient, value_up_gradient, mid = attention(
        n, projected, down_projected[:, :rank], down_projected[:, rank:2 * rank],
        query_up_adapter, value_up_adapter, grad_rows,
    )
    query_cols = query_up_gradient.shape[1]
    down_gradient, up_gradient = finish(
        sizes, mid, own, jnp.concatenate([query_up_gradient, value_up_gradient], 1), 2 * rank
    )
    down_gradient = down_gradient.T
    return (
        out_rows[None],
        down_gradient[:, :rank],
        up_gradient[:, :query_cols],
        down_gradient[:, rank:],
        up_gradient[:, query_cols:],
    )


def solution(mesh):
    sizes = (mesh.shape["tensor"], mesh.shape["dp"] // CORES, mesh.shape["fsdp"])
    return jax.shard_map(
        functools.partial(local, sizes),
        mesh=mesh,
        in_specs=(
            P(("dp", "fsdp"), "tensor", None),
            P(),
            P(("dp", "fsdp"), "tensor"),
            P(),
            P(None, "tensor"),
            P(),
            P(None, "tensor"),
            P(("dp", "fsdp"), "tensor", None),
        ),
        out_specs=(
            P(("dp", "fsdp"), "tensor", None),
            P(),
            P(None, "tensor"),
            P(),
            P(None, "tensor"),
        ),
        check_vma=False,
    )
```

time: 611 us -> 346 us (0.57)
  waiting for transfers between devices: 343 us -> 0 us
  Pallas kernels: 31 us -> 325 us
  blocking collectives: 101 us -> 0 us
  matrix products: 74.4 us -> 0 us
  starting transfers between devices: 20.1 us -> 0 us
  between operations: 14.1 us -> 0.76 us
  local copies, waits for them, and re-layouts: 20.6 us -> 8.82 us
    pallas_call x1 -> x3, Pallas kernels: 31 us -> 325 us  [the longest x1 247 us: project(): pl.pallas_call(functools.partial(project_kernel, n, chips, fsdp), in_spec...]
    psum x2 -> x0, waiting for transfers between devices: 178 us -> none  [the longest x1 128 us: local(): down_gradient = lax.psum(down_gradient, ('dp', 'fsdp', 'tensor')).T]
    ppermute x6 -> x0, waiting for transfers between devices: 145 us -> none  [the longest x3 79.1 us: local(): lax.ppermute(down_block, 'tensor', [(i, i - 1) for i in range(1, count -...]
    all_gather x1 -> x0, blocking collectives: 85.9 us -> none  [local(): down_projected = lax.all_gather(down_own, 'tensor', axis=0, tiled=True)]
    dot_general x9 -> x0, matrix products: 74.4 us -> none  [the longest x7 67.9 us: local(): jnp.dot(rows, weights, preferred_element_type=jnp.float32)]
    unnamed x5 -> x0, waiting for transfers between devices: 20.3 us -> none
    psum x1 -> x0, blocking collectives: 14.8 us -> none  [local(): lax.psum((query_up_gradient, value_up_gradient), ('dp', 'fsdp'))]
    ppermute x6 -> x0, starting transfers between devices: 12.8 us -> none  [the longest x3 8.46 us: local(): lax.ppermute(up_block, 'tensor', [(i, i + 1) for i in range(step - 1, cou...]
  transfers between devices with their start and end apart: 12 -> 0, of which waited for: 7 -> 0; matrix products, arithmetic and copies ran while one was open for 14% -> 0% of each run, Pallas kernels for 0% -> 0%
where the time goes in v1:
time: 346 us
  Pallas kernels  325 us (94%)
  other arithmetic  11.3 us (3%)
  local copies, waits for them, and re-layouts  8.82 us (3%)
    pallas_call x1, Pallas kernels, project(): pl.pallas_call(functools.partial(project_kernel, n, chips, fsdp), in_spec...  247 us
    pallas_call x1, Pallas kernels, attention(): pl.pallas_call(functools.partial(attention_kernel, block, n), grid=(group...  41.3 us
    pallas_call x1, Pallas kernels, finish(): pl.pallas_call(functools.partial(finish_kernel, n, chips, fsdp), in_specs...  36 us

profile of v1, /device:TPU:0, one launch (start us, length us, event | category | flops | bytes accessed | tf_op | source)
XLA Modules:
  0.0 345.8 jit_solution(8247230595074202752)
XLA Ops:
  0.6 0.1 pad.8.clone
  0.7 2.7 fusion
  3.4 1.5 fusion.5
  4.9 0.3 pad_maximum_fusion
  5.2 0.0 copy-done.5
  5.2 1.0 copy.13
  6.2 0.0 copy-done.6
  6.2 1.7 copy.14
  8.0 4.4 %maximum_maximum_fusion.adp_ref = bf16[8192,128]{1,0:T(8,128)(2,1)} fusion(bf16[8192,16]{1,0:T(8,128)(2,1)} %copy.14, bf16[8192,16]{1,0:T(8,128)(2,1)S(1)} %copy.13, bf16[128]{0:T(256)(128)(2,1)S(1)} %pad.8.clone), kind=kLoop, calls=%fused_computation.5 | loop fusion | flops 6291456 | bytes 2621696 | tf_op jit(solution)/shard_map/concatenate | solution.py:690
  12.3 0.0 copy-done.4
  12.3 0.0 copy-done.7
  12.3 2.5 fusion.2.tok_ref.own_ref
  14.9 247.5 %project.1 = (f32[768,1280]{1,0:T(8,128)}, bf16[768,128]{1,0:T(8,128)(2,1)}, bf16[768,1024]{1,0:T(8,128)(2,1)}) custom-call(bf16[192,8192]{1,0:T(8,128)(2,1)} %fusion.2.tok_ref.own_ref, bf16[1024,1280]{1,0:T(8,128)(2,1)} %w_ref.1, bf16[8192,128]{1,0:T(8,128)(2,1)} %maximum_maximum_fusion.adp_ref, bf16[192,4096]{1,0:T(8,128)(2,1)} %bitcast.9), custom_call_target="tpu_custom_call" | custom-call | flops 16106127360 | bytes 20971520 | tf_op jit(solution)/shard_map/project/pallas_call | solution.py:298
  262.4 1.1 fusion.7
  263.5 0.0 copy-done.1
  263.6 0.0 copy-done.2
  263.6 0.0 copy-start.3
  263.6 1.4 copy-done.3
  265.0 41.3 %attention.1 = (bf16[192,4096]{1,0:T(8,128)(2,1)S(1)}, f32[16,1024]{1,0:T(8,128)S(1)}, f32[16,128]{1,0:T(8,128)S(1)}, f32[768,128]{1,0:T(8,128)S(1)}) custom-call(f32[768,1280]{1,0:T(8,128)} %get-tuple-element.14.q_ref.k_ref.v_ref, f32[768,1280]{1,0:T(8,128)} %get-tuple-element.14.q_ref.k_ref.v_ref, f32[768,1280]{1,0:T(8,128)} %get-tuple-element.14.q_ref.k_ref.v_ref, ...), custom_call_target="tpu_custom_call" | custom-call | flops 6039797760 | bytes 7077888 | tf_op jit(solution)/shard_map/attention/pallas_call | solution.py:441
  306.3 36.0 %finish.1 = (f32[32,8192]{1,0:T(8,128)S(1)}, f32[16,1152]{1,0:T(8,128)S(1)}) custom-call(f32[768,128]{1,0:T(8,128)S(1)} %get-tuple-element.18.mid_ref, bf16[192,8192]{1,0:T(8,128)(2,1)S(1)} %copy-done, f32[16,1152]{1,0:T(8,128)S(1)} %pad_maximum_fusion.2.gb_ref), custom_call_target="tpu_custom_call" | custom-call | flops 402653184 | bytes 3145728 | tf_op jit(solution)/shard_map/finish/pallas_call | solution.py:648
  342.3 1.0 fusion.6
  343.4 0.6 slice.23
  344.0 0.6 slice.21
  344.6 1.1 copy.16
  (12 shorter events, 0.0 us)
Async XLA Ops:
  0.7 4.4 %copy-start.5 = (bf16[8192,16]{0,1:T(8,128)(2,1)S(1)}, bf16[8192,16]{0,1:T(8,128)(2,1)}, u32[]{:S(2)}) copy-start(bf16[8192,16]{0,1:T(8,128)(2,1)} %param.11) | copy-start | bytes 786436
  3.4 2.8 copy-start.6
  7.9 4.4 %copy-start.4 = (bf16[1,192,8192]{2,1,0:T(8,128)(2,1)S(1)}, bf16[1,192,8192]{2,1,0:T(8,128)(2,1)}, u32[]{:S(2)}) copy-start(bf16[1,192,8192]{2,1,0:T(8,128)(2,1)} %param.8) | copy-start | bytes 9437188
  8.0 4.4 %copy-start.7 = (f32[8192]{0:T(1024)S(1)}, f32[8192]{0:T(1024)}, u32[]{:S(2)}) copy-start(f32[8192]{0:T(1024)} %param.9) | copy-start | bytes 98308
  14.9 248.7 %copy-start.1 = (bf16[16,1024]{1,0:T(8,128)(2,1)S(1)}, bf16[16,1024]{1,0:T(8,128)(2,1)}, u32[]{:S(2)}) copy-start(bf16[16,1024]{1,0:T(8,128)(2,1)} %qup_ref.1) | copy-start | bytes 98308
  14.9 248.7 %copy-start.2 = (bf16[16,128]{1,0:T(8,128)(2,1)S(1)}, bf16[16,128]{1,0:T(8,128)(2,1)}, u32[]{:S(2)}) copy-start(bf16[16,128]{1,0:T(8,128)(2,1)} %vup_ref.1) | copy-start | bytes 12292
  263.6 1.4 copy-start.3
  265.0 41.4 %copy-start = (bf16[192,8192]{1,0:T(8,128)(2,1)S(1)}, bf16[192,8192]{1,0:T(8,128)(2,1)}, u32[]{:S(2)}) copy-start(bf16[192,8192]{1,0:T(8,128)(2,1)} %fusion.2.tok_ref.own_ref) | copy-start | bytes 9437188
